TPU v7x, 32 devices: a whole 2x2x4 slice. The times are simulated.
32 devices in a mesh: groups: 2 (over y), seq: 4 (over z), tensor: 2 (over x), sub: 2 (over core).
Axes of the slice: x: 2, y: 2, z: 4, core: 2. Of those that a mesh axis runs over, the one named last changes fastest.
Arguments:
- image_tokens: bfloat16 [2048, 3072], P(('groups', 'seq')), parts along dimension 0, may hold values from -6 to 6
- text_tokens: bfloat16 [256, 3072], P(('groups', 'seq')), parts along dimension 0, may hold values from -6 to 6
- timestep: int32 [2], P('groups'), parts along dimension 0, may hold values from 0 to 49
- text_length: int32 [2], P('groups'), parts along dimension 0, may hold values from 32 to 128
- time_table: bfloat16 [50, 3072], replicated, may hold values from -6 to 6
- mod_weight: bfloat16 [3072, 18432], P('seq', ('tensor', 'sub')), may hold values from -0.109375 to 0.109375
- qkv_image: bfloat16 [3072, 6144], P('seq', ('tensor', 'sub')), as said below
- qkv_text: bfloat16 [3072, 6144], P('seq', ('tensor', 'sub')), as said below
- norm_gain: float32 [2, 2, 16, 128], P(None, None, ('tensor', 'sub')), may hold values from 1 to 6
- proj_image: bfloat16 [2048, 3072], P(('tensor', 'sub'), 'seq'), may hold values from -0.125 to 0.125
- proj_text: bfloat16 [2048, 3072], P(('tensor', 'sub'), 'seq'), may hold values from -0.125 to 0.125
Outputs:
- image_out: bfloat16 [2048, 3072], P(('groups', 'seq'), ('tensor', 'sub')), parts along dimension 0
- text_out: bfloat16 [256, 3072], P(('groups', 'seq'), ('tensor', 'sub')), parts along dimension 0
There are 2 independent parts, one for each index of `groups`. A program takes and returns all parts, laid end to end along the dimension named above; an argument that names none is the same for every part. Nothing has to cross between parts.
Inputs may be any that keep to these rules, and one draw needn't show every extreme that they name: `qkv_image`: entries of standard deviation about 1/sqrt(3072). `qkv_text`: entries of standard deviation about 1/sqrt(3072).
All inputs are finite; a program needn't handle non-finite values.
Results may differ from a plain program's by a relative error of at most 0.0085.
Values may be sent and summed in bfloat16 or wider, within the bound.
No kernel may reach another device: no remote copies, remote signals or barrier semaphores. Data moves between devices by JAX's collectives and lax.ppermute only.
A program may use at most 64 MiB of HBM per device.

v0:
```python
import jax
import jax.numpy as jnp
from jax import lax
from jax.sharding import PartitionSpec as P

EPSILON = 1e-06


def modulate(tokens, shift, scaling):
    values = tokens.astype(jnp.float32)
    center = jnp.mean(values, axis=-1, keepdims=True)
    spread = jnp.mean(jnp.square(values - center), axis=-1, keepdims=True)
    normed = (values - center) * lax.rsqrt(spread + EPSILON)
    return (normed * (1.0 + scaling) + shift).astype(jnp.bfloat16)


def head_norm(values, gain):
    return values * lax.rsqrt(jnp.mean(values * values, axis=-1, keepdims=True) + EPSILON) * gain


def split_heads(projected, gains):
    shaped = projected.reshape(projected.shape[0], -1, 3, gains.shape[-1])
    queries = head_norm(shaped[:, :, 0], gains[0]).astype(jnp.bfloat16)
    keys = head_norm(shaped[:, :, 1], gains[1]).astype(jnp.bfloat16)
    values = shaped[:, :, 2].astype(jnp.bfloat16)
    return (queries, keys, values)


def add_rows(source, shards):
    return jnp.dot(source, shards, preferred_element_type=jnp.float32)


def body(
    image_tokens,
    text_tokens,
    timestep,
    text_length,
    time_table,
    mod_weight,
    qkv_image,
    qkv_text,
    norm_gain,
    proj_image,
    proj_text,
):
    columns_all = image_tokens.shape[1]
    embedded = lax.dynamic_index_in_dim(time_table, timestep[0], 0, keepdims=False).astype(
        jnp.float32
    )
    vector = jax.nn.silu(embedded).astype(jnp.bfloat16)
    slab_rows = mod_weight.shape[0]
    vector_rows = lax.dynamic_slice_in_dim(vector, lax.axis_index("seq") * slab_rows, slab_rows)
    partial_value = jnp.dot(vector_rows[None, :], mod_weight, preferred_element_type=jnp.float32)[0]
    summed_rows = lax.psum(partial_value, "seq")
    modulation = lax.all_gather(summed_rows, ("tensor", "sub"), axis=0, tiled=True)
    modulation = modulation.reshape(2, 3, columns_all)
    hidden_image = modulate(image_tokens, modulation[0, 0], modulation[0, 1])
    hidden_text = modulate(text_tokens, modulation[1, 0], modulation[1, 1])
    image_count = image_tokens.shape[0]
    text_count = text_tokens.shape[0]
    local_rows = image_count + text_count
    projected_image = add_rows(hidden_image, lax.all_gather(qkv_image, "seq", axis=0, tiled=True))
    projected_text = add_rows(hidden_text, lax.all_gather(qkv_text, "seq", axis=0, tiled=True))
    image_q, image_k, image_v = split_heads(projected_image, norm_gain[0])
    text_q, text_k, text_v = split_heads(projected_text, norm_gain[1])
    heads_here = image_q.shape[1]
    head_size = image_q.shape[2]
    queries = jnp.concatenate([text_q, image_q], axis=0)
    keys = jnp.concatenate([text_k, image_k], axis=0)
    values = jnp.concatenate([text_v, image_v], axis=0)
    keys_values = jnp.stack([keys, values], axis=2).reshape(local_rows, heads_here * 2 * head_size)
    factor = float(head_size) ** (-0.5)
    shards = lax.all_gather(keys_values, "seq", axis=0, tiled=True)
    count = shards.shape[0]
    blocks = shards.reshape(count, heads_here, 2, head_size)
    position = jnp.arange(count, dtype=jnp.int32)
    within = position % local_rows
    owner = position // local_rows
    usable = (within >= text_count) | (owner * text_count + within < text_length[0])
    scores = (
        jnp.einsum("qhd,khd->hqk", queries, blocks[:, :, 0], preferred_element_type=jnp.float32)
        * factor
    )
    scores = jnp.where(usable[None, None, :], scores, -1e30)
    run_max = jnp.full((heads_here, local_rows), -1e30, jnp.float32)
    new_max = jnp.maximum(run_max, jnp.max(scores, axis=-1))
    probs = jnp.exp(scores - new_max[:, :, None])
    run_sum = jnp.sum(probs, axis=-1)
    totals = jnp.einsum(
        "hqk,khd->hqd",
        probs.astype(jnp.bfloat16),
        blocks[:, :, 1],
        preferred_element_type=jnp.float32,
    )
    final_max, run_sum, totals = (new_max, run_sum, totals)
    attended = (
        (totals / run_sum[:, :, None])
        .astype(jnp.bfloat16)
        .transpose(1, 0, 2)
        .reshape(local_rows, heads_here * head_size)
    )
    stacked = jnp.stack([proj_image, proj_text], axis=0)
    text_attended = attended[:text_count]
    image_attended = attended[text_count:]
    shards = lax.all_gather(stacked, "seq", axis=2, tiled=True)
    text_part = jnp.dot(text_attended, shards[1], preferred_element_type=jnp.float32)
    image_part = jnp.dot(image_attended, shards[0], preferred_element_type=jnp.float32)
    branch = jnp.concatenate([text_part, image_part], axis=0)
    summed = lax.psum_scatter(
        branch.astype(jnp.bfloat16), ("tensor", "sub"), scatter_dimension=1, tiled=True
    ).astype(jnp.float32)
    width_here = summed.shape[1]
    first = lax.axis_index(("tensor", "sub")) * width_here
    gates = lax.dynamic_slice_in_dim(modulation[:, 2], first, width_here, 1)
    image_base = lax.dynamic_slice_in_dim(image_tokens, first, width_here, 1).astype(jnp.float32)
    text_base = lax.dynamic_slice_in_dim(text_tokens, first, width_here, 1).astype(jnp.float32)
    image_out = (image_base + gates[0] * summed[text_count:]).astype(jnp.bfloat16)
    text_out = (text_base + gates[1] * summed[:text_count]).astype(jnp.bfloat16)
    return (image_out, text_out)


def solution(mesh):
    return jax.shard_map(
        body,
        mesh=mesh,
        in_specs=(
            P(("groups", "seq"), None),
            P(("groups", "seq"), None),
            P("groups"),
            P("groups"),
            P(),
            P("seq", ("tensor", "sub")),
            P("seq", ("tensor", "sub")),
            P("seq", ("tensor", "sub")),
            P(None, None, ("tensor", "sub"), None),
            P(("tensor", "sub"), "seq"),
            P(("tensor", "sub"), "seq"),
        ),
        out_specs=(
            P(("groups", "seq"), ("tensor", "sub")),
            P(("groups", "seq"), ("tensor", "sub")),
        ),
        check_vma=False,
    )
```

profile of v0, /device:TPU:0, one launch (start us, length us, event | category | flops | bytes accessed | tf_op | source)
XLA Modules:
  0.0 563.6 jit_solution(5315166292770970705)
XLA Ops:
  10.3 4.2 convolution_reduce_fusion
  14.5 27.8 %psum.7 = f32[4608]{0:T(1024)S(1)} all-reduce(f32[4608]{0:T(1024)S(1)} %convolution_reduce_fusion), channel_id=1, replica_groups=mesh['groups'=2,'seq'=4,'tensor'=2,'sub'=2] {'seq'}, use_global_device_ids=true, to_apply=%region_0.1 | all-reduce | flops 4608 | bytes 36864 | tf_op jit(solution)/shard_map/psum | solution.py:54
  42.3 5.3 all-gather
  49.2 130.5 %all-gather.8.cloned.1.call-done = bf16[3072,1536]{1,0:T(8,128)(2,1)} async-done(((bf16[768,1536]{1,0:T(8,128)(2,1)}), bf16[3072,1536]{1,0:T(8,128)(2,1)}) %all-gather.8.cloned.1.call-update) | async-done | bytes 9437200 | tf_op jit(solution)/shard_map/all_gather | solution.py:62
  179.6 6.8 %fusion.11 = f32[256,1536]{0,1:T(8,128)S(1)} fusion(bf16[3072,1536]{1,0:T(8,128)(2,1)} %all-gather.8.cloned.1.call-done, bf16[256,3072]{1,0:T(8,128)(2,1)S(1)} %copy-done, f32[3072]{0:T(1024)S(1)} %bitcast.108, f32[3072]{0:T(1024)S(1)} %bitcast.109, f32[256]{0:T(256)S(1)} %add_rsqrt_fusion.4, f32[256]{0:T(256)S(1)} %broadcast_multiply_fusion), kind=kOutput, calls=%fused_computation.19 | convolution fusion | flops 2420637696 | bytes 12609536 | tf_op jit(solution)/shard_map/dot_general | solution.py:30
  186.5 1.1 copy-done.3
  187.6 158.6 %all-gather.6.cloned.1.call-done = bf16[3072,1536]{1,0:T(8,128)(2,1)} async-done(((bf16[768,1536]{1,0:T(8,128)(2,1)}), bf16[3072,1536]{1,0:T(8,128)(2,1)}) %all-gather.6.cloned.1.call-update) | async-done | bytes 9437200 | tf_op jit(solution)/shard_map/all_gather | solution.py:63
  346.2 5.5 fusion.41
  352.5 1.2 multiply_convert_fusion
  355.0 1.3 reshape.144
  356.3 2.6 pad_maximum_fusion.1
  359.9 1.1 slice.128
  361.8 42.8 %all-gather.10.cloned.1.call-done = bf16[1152,1024]{1,0:T(8,128)(2,1)} async-done(((bf16[288,1024]{1,0:T(8,128)(2,1)}), bf16[1152,1024]{1,0:T(8,128)(2,1)}) %all-gather.10.cloned.1.call-update) | async-done | bytes 2359312 | tf_op jit(solution)/shard_map/all_gather | solution.py:73
  404.6 4.3 copy.59
  408.9 2.3 fusion.63
  411.2 1.1 fusion
  413.1 1.0 fusion.23
  414.3 105.8 %all-gather.12.cloned.1.call-done = bf16[2,512,3072]{2,1,0:T(8,128)(2,1)} async-done(((bf16[2,512,768]{2,1,0:T(8,128)(2,1)}), bf16[2,512,3072]{2,1,0:T(8,128)(2,1)}) %all-gather.12.cloned.1.call-update) | async-done | bytes 6291472 | tf_op jit(solution)/shard_map/all_gather | solution.py:105
  520.1 2.5 convolution_convert_fusion.1
  522.7 2.9 convolution_convert_fusion
  525.6 1.3 pad_maximum_fusion
  527.0 27.5 %reduce-scatter.2.cloned.1.call-done = bf16[288,768]{1,0:T(8,128)(2,1)} async-done(((bf16[288,3072]{1,0:T(8,128)(2,1)}), bf16[288,768]{1,0:T(8,128)(2,1)}) %reduce-scatter.2.cloned.1.call-update) | async-done | bytes 442384 | tf_op jit(solution)/shard_map/reduce_scatter | solution.py:109
  554.5 1.1 convert_element_type.80
  555.6 0.9 fusion.27
  (63 shorter events, 8.9 us)
Async XLA Ops:
  7.2 172.5 %all-gather.8.cloned.1.call-start = ((), (), s32[]{:S(2)}) async-start(), calls=%async_computation.2 | async-start | bytes 11796480 | tf_op jit(solution)/shard_map/all_gather | solution.py:62
  7.9 338.3 %all-gather.6.cloned.1.call-start = ((), (), s32[]{:S(2)}) async-start(), calls=%async_computation.1 | async-start | bytes 11796480 | tf_op jit(solution)/shard_map/all_gather | solution.py:63
  8.6 395.9 %all-gather.10.cloned.1.call-start = ((), (), s32[]{:S(2)}) async-start(), calls=%async_computation.3 | async-start | bytes 2949120 | tf_op jit(solution)/shard_map/all_gather | solution.py:73
  10.3 37.6 %copy-start.2 = (bf16[32,3072]{1,0:T(8,128)(2,1)S(1)}, bf16[32,3072]{1,0:T(8,128)(2,1)}, u32[]{:S(2)}) copy-start(bf16[32,3072]{1,0:T(8,128)(2,1)} %param.12) | copy-start | bytes 589828
  10.3 37.9 %copy-start = (bf16[256,3072]{1,0:T(8,128)(2,1)S(1)}, bf16[256,3072]{1,0:T(8,128)(2,1)}, u32[]{:S(2)}) copy-start(bf16[256,3072]{1,0:T(8,128)(2,1)} %param.11) | copy-start | bytes 4718596
  14.5 34.6 %copy-start.4 = (f32[2,2,4,128]{3,2,1,0:T(4,128)S(1)}, f32[2,2,4,128]{3,2,1,0:T(4,128)}, u32[]{:S(2)}) copy-start(f32[2,2,4,128]{3,2,1,0:T(4,128)} %param.19) | copy-start | bytes 24580
  186.4 1.2 copy-start.3
  356.3 163.9 %all-gather.12.cloned.1.call-start = ((), (), s32[]{:S(2)}) async-start(), calls=%async_computation.4 | async-start | bytes 7864320 | tf_op jit(solution)/shard_map/all_gather | solution.py:105
  359.0 195.5 %reduce-scatter.2.cloned.1.call-start = ((), (), s32[]{:S(2)}) async-start(), calls=%async_computation.5 | async-start | bytes 2211840 | tf_op jit(solution)/shard_map/reduce_scatter | solution.py:109
  411.2 1.9 copy-start.1
Sparse Core Ops, SparseCore 0:
  9.5 170.0 all-gather.7
  181.2 164.9 all-gather.5
  356.4 48.1 all-gather.9
  406.0 114.0 all-gather.11
  527.0 27.4 reduce-scatter.1
where the time goes:
time: 564 us
  waiting for transfers between devices  467 us (83%)
  blocking collectives  33.1 us (6%)
  matrix products  25.1 us (4%)
  between operations  15.4 us (3%)
  other arithmetic  12.6 us (2%)
  local copies, waits for them, and re-layouts  10.4 us (2%)
    all_gather x1, waiting for transfers between devices, body(): lax.all_gather(qkv_text, 'seq', axis=0, tiled=True)  159 us
    all_gather x1, waiting for transfers between devices, body(): lax.all_gather(qkv_image, 'seq', axis=0, tiled=True)  130 us
    all_gather x1, waiting for transfers between devices, body(): shards = lax.all_gather(stacked, 'seq', axis=2, tiled=True)  106 us
    all_gather x1, waiting for transfers between devices, body(): shards = lax.all_gather(keys_values, 'seq', axis=0, tiled=True)  42.8 us
    psum x1, blocking collectives, body(): summed_rows = lax.psum(partial_value, 'seq')  27.8 us
    reduce_scatter x1, waiting for transfers between devices, body(): lax.psum_scatter(branch.astype(jnp.bfloat16), ('tensor', 'sub'), scatter_...  27.5 us
    dot_general x2, matrix products, add_rows(): return jnp.dot(source, shards, preferred_element_type=jnp.float32)  12.2 us
  transfers between devices with their start and end apart: 5, of which 5 were waited for; matrix products, arithmetic and copies ran while one was open for 5% of the time, Pallas kernels for 0%

commit v1 on v0

--- a/solution.py
+++ b/solution.py
@@ -70,7 +70,12 @@
     values = jnp.concatenate([text_v, image_v], axis=0)
     keys_values = jnp.stack([keys, values], axis=2).reshape(local_rows, heads_here * 2 * head_size)
     factor = float(head_size) ** (-0.5)
-    shards = lax.all_gather(keys_values, "seq", axis=0, tiled=True)
+    ring = [keys_values]
+    for hop in range(3):
+        ring.append(lax.ppermute(ring[-1], "seq", [(dev, (dev + 1) % 4) for dev in range(4)]))
+    shards = jnp.roll(
+        jnp.concatenate(ring[::-1], axis=0), (lax.axis_index("seq") + 1) * ring[0].shape[0], axis=0
+    )
     count = shards.shape[0]
     blocks = shards.reshape(count, heads_here, 2, head_size)
     position = jnp.arange(count, dtype=jnp.int32)

time: 564 us -> 544 us (0.965)
  waiting for transfers between devices: 467 us -> 427 us
  starting transfers between devices: 0.38 us -> 25 us
    ppermute x0 -> x3, waiting for transfers between devices: none -> 80.1 us  [body(): lax.ppermute(ring[-1], 'seq', [(dev, (dev + 1) % 4) for dev in range(4)])]
    all_gather x1, waiting for transfers between devices: 106 us -> 27.2 us  [body(): shards = lax.all_gather(stacked, 'seq', axis=2, tiled=True)]
    all_gather x1 -> x0, waiting for transfers between devices: 42.8 us -> none  [body(): shards = lax.all_gather(keys_values, 'seq', axis=0, tiled=True)]
    all_gather x1, waiting for transfers between devices: 130 us -> 160 us  [body(): lax.all_gather(qkv_image, 'seq', axis=0, tiled=True)]
    all_gather x1, waiting for transfers between devices: 159 us -> 130 us  [body(): lax.all_gather(qkv_text, 'seq', axis=0, tiled=True)]
    ppermute x0 -> x3, starting transfers between devices: none -> 24.8 us  [body(): lax.ppermute(ring[-1], 'seq', [(dev, (dev + 1) % 4) for dev in range(4)])]
  transfers between devices with their start and end apart: 5 -> 7, of which waited for: 5 -> 7; matrix products, arithmetic and copies ran while one was open for 5% -> 6% of each run, Pallas kernels for 0% -> 0%
where the time goes in v1:
time: 544 us
  waiting for transfers between devices  427 us (78%)
  blocking collectives  32 us (6%)
  matrix products  25.1 us (5%)
  starting transfers between devices  25 us (5%)
  between operations  15.5 us (3%)
  other arithmetic  11.3 us (2%)
  local copies, waits for them, and re-layouts  7.94 us (1%)
    all_gather x1, waiting for transfers between devices, body(): lax.all_gather(qkv_image, 'seq', axis=0, tiled=True)  160 us
    all_gather x1, waiting for transfers between devices, body(): lax.all_gather(qkv_text, 'seq', axis=0, tiled=True)  130 us
    ppermute x3, waiting for transfers between devices, body(): lax.ppermute(ring[-1], 'seq', [(dev, (dev + 1) % 4) for dev in range(4)])  80.1 us
    reduce_scatter x1, waiting for transfers between devices, body(): lax.psum_scatter(branch.astype(jnp.bfloat16), ('tensor', 'sub'), scatter_...  27.5 us
    all_gather x1, waiting for transfers between devices, body(): shards = lax.all_gather(stacked, 'seq', axis=2, tiled=True)  27.2 us
    psum x1, blocking collectives, body(): summed_rows = lax.psum(partial_value, 'seq')  26.7 us
    ppermute x3, starting transfers between devices, body(): lax.ppermute(ring[-1], 'seq', [(dev, (dev + 1) % 4) for dev in range(4)])  24.8 us
    dot_general x2, matrix products, add_rows(): return jnp.dot(source, shards, preferred_element_type=jnp.float32)  12.2 us
  transfers between devices with their start and end apart: 7, of which 7 were waited for; matrix products, arithmetic and copies ran while one was open for 6% of the time, Pallas kernels for 0%

profile of v1, /device:TPU:0, one launch (start us, length us, event | category | flops | bytes accessed | tf_op | source)
XLA Modules:
  0.0 543.7 jit_solution(3345285950190533545)
XLA Ops:
  8.7 1.4 pad_maximum_fusion.1
  11.8 4.2 convolution_reduce_fusion
  16.0 26.7 %psum.7 = f32[4608]{0:T(1024)S(1)} all-reduce(f32[4608]{0:T(1024)S(1)} %convolution_reduce_fusion), channel_id=1, replica_groups=mesh['groups'=2,'seq'=4,'tensor'=2,'sub'=2] {'seq'}, use_global_device_ids=true, to_apply=%region_0.1 | all-reduce | flops 4608 | bytes 36864 | tf_op jit(solution)/shard_map/psum | solution.py:54
  43.4 5.3 all-gather
  49.6 130.2 %all-gather.5.cloned.1.call-done = bf16[3072,1536]{1,0:T(8,128)(2,1)} async-done(((bf16[768,1536]{1,0:T(8,128)(2,1)}), bf16[3072,1536]{1,0:T(8,128)(2,1)}) %all-gather.5.cloned.1.call-update) | async-done | bytes 9437200 | tf_op jit(solution)/shard_map/all_gather | solution.py:63
  179.7 5.5 %fusion.41 = f32[32,1536]{1,0:T(8,128)S(1)} fusion(bf16[3072,1536]{1,0:T(8,128)(2,1)} %all-gather.5.cloned.1.call-done, bf16[32,3072]{1,0:T(8,128)(2,1)S(1)} %copy-done.2, f32[3072]{0:T(1024)S(1)} %bitcast.106, f32[3072]{0:T(1024)S(1)} %bitcast.105, f32[32]{0:T(128)S(1)} %add_rsqrt_fusion.5, f32[32]{0:T(128)S(1)} %broadcast_multiply_fusion.1), kind=kOutput, calls=%fused_computation.58 | convolution fusion | flops 302579712 | bytes 9855232 | tf_op jit(solution)/shard_map/dot_general | solution.py:30
  186.0 160.4 %all-gather.7.cloned.1.call-done = bf16[3072,1536]{1,0:T(8,128)(2,1)} async-done(((bf16[768,1536]{1,0:T(8,128)(2,1)}), bf16[3072,1536]{1,0:T(8,128)(2,1)}) %all-gather.7.cloned.1.call-update) | async-done | bytes 9437200 | tf_op jit(solution)/shard_map/all_gather | solution.py:62
  346.5 6.8 %fusion.11 = f32[256,1536]{0,1:T(8,128)S(1)} fusion(bf16[3072,1536]{1,0:T(8,128)(2,1)} %all-gather.7.cloned.1.call-done, bf16[256,3072]{1,0:T(8,128)(2,1)S(1)} %copy-done, f32[3072]{0:T(1024)S(1)} %bitcast.108, f32[3072]{0:T(1024)S(1)} %bitcast.109, f32[256]{0:T(256)S(1)} %add_rsqrt_fusion.4, f32[256]{0:T(256)S(1)} %broadcast_multiply_fusion), kind=kOutput, calls=%fused_computation.19 | convolution fusion | flops 2420637696 | bytes 12609536 | tf_op jit(solution)/shard_map/dot_general | solution.py:30
  355.7 30.3 %collective-permute-done = bf16[288,1024]{1,0:T(8,128)(2,1)S(1)} collective-permute-done((bf16[288,1024]{1,0:T(8,128)(2,1)S(1)}, bf16[288,1024]{1,0:T(8,128)(2,1)S(1)}, u32[]{:S(2)}, u32[]{:S(2)}) %collective-permute-start) | collective-permute-done | bytes 589856 | tf_op jit(solution)/shard_map/ppermute | solution.py:75
  386.0 8.5 %collective-permute-start.1 = (bf16[288,1024]{1,0:T(8,128)(2,1)S(1)}, bf16[288,1024]{1,0:T(8,128)(2,1)S(1)}, u32[]{:S(2)}, u32[]{:S(2)}) collective-permute-start(bf16[288,1024]{1,0:T(8,128)(2,1)S(1)} %collective-permute-done), channel_id=1, source_target_pairs={{0,4},{4,8},{8,12},{12,0},{1,5},{5,9},{9,13},{13,1},{2,6},{6,10},{... | collective-permute-start | bytes 1769480 | tf_op jit(solution)/shard_map/ppermute | solution.py:75
  395.2 1.1 slice.128
  396.8 23.2 %collective-permute-done.1 = bf16[288,1024]{1,0:T(8,128)(2,1)S(1)} collective-permute-done((bf16[288,1024]{1,0:T(8,128)(2,1)S(1)}, bf16[288,1024]{1,0:T(8,128)(2,1)S(1)}, u32[]{:S(2)}, u32[]{:S(2)}) %collective-permute-start.1) | collective-permute-done | bytes 589856 | tf_op jit(solution)/shard_map/ppermute | solution.py:75
  420.0 16.3 %collective-permute-start.2 = (bf16[288,1024]{1,0:T(8,128)(2,1)S(1)}, bf16[288,1024]{1,0:T(8,128)(2,1)S(1)}, u32[]{:S(2)}, u32[]{:S(2)}) collective-permute-start(bf16[288,1024]{1,0:T(8,128)(2,1)S(1)} %collective-permute-done.1), channel_id=1, source_target_pairs={{0,4},{4,8},{8,12},{12,0},{1,5},{5,9},{9,13},{13,1},{2,6},{6,10},{... | collective-permute-start | bytes 1769480 | tf_op jit(solution)/shard_map/ppermute | solution.py:75
  436.6 26.7 %collective-permute-done.2 = bf16[288,1024]{1,0:T(8,128)(2,1)S(1)} collective-permute-done((bf16[288,1024]{1,0:T(8,128)(2,1)S(1)}, bf16[288,1024]{1,0:T(8,128)(2,1)S(1)}, u32[]{:S(2)}, u32[]{:S(2)}) %collective-permute-start.2) | collective-permute-done | bytes 589856 | tf_op jit(solution)/shard_map/ppermute | solution.py:75
  464.3 2.6 copy.59
  466.8 2.3 fusion.63
  469.2 1.1 fusion
  472.0 27.2 %all-gather.9.cloned.1.call-done = bf16[2,512,3072]{2,1,0:T(8,128)(2,1)} async-done(((bf16[2,512,768]{2,1,0:T(8,128)(2,1)}), bf16[2,512,3072]{2,1,0:T(8,128)(2,1)}) %all-gather.9.cloned.1.call-update) | async-done | bytes 6291472 | tf_op jit(solution)/shard_map/all_gather | solution.py:110
  499.2 2.5 convolution_convert_fusion.1
  501.8 2.9 convolution_convert_fusion
  504.7 1.3 pad_maximum_fusion
  506.1 27.5 %reduce-scatter.2.cloned.1.call-done = bf16[288,768]{1,0:T(8,128)(2,1)} async-done(((bf16[288,3072]{1,0:T(8,128)(2,1)}), bf16[288,768]{1,0:T(8,128)(2,1)}) %reduce-scatter.2.cloned.1.call-update) | async-done | bytes 442384 | tf_op jit(solution)/shard_map/reduce_scatter | solution.py:114
  533.6 1.1 convert_element_type.80
  535.3 1.8 fusion.27
  (79 shorter events, 11.5 us)
Async XLA Ops:
  7.2 1.6 copy-start.5
  7.2 1.6 copy-start.4
  7.2 172.5 %all-gather.5.cloned.1.call-start = ((), (), s32[]{:S(2)}) async-start(), calls=%async_computation.1 | async-start | bytes 11796480 | tf_op jit(solution)/shard_map/all_gather | solution.py:63
  7.9 338.5 %all-gather.7.cloned.1.call-start = ((), (), s32[]{:S(2)}) async-start(), calls=%async_computation.2 | async-start | bytes 11796480 | tf_op jit(solution)/shard_map/all_gather | solution.py:62
  8.7 490.6 %all-gather.9.cloned.1.call-start = ((), (), s32[]{:S(2)}) async-start(), calls=%async_computation.3 | async-start | bytes 7864320 | tf_op jit(solution)/shard_map/all_gather | solution.py:110
  10.1 523.5 %reduce-scatter.2.cloned.1.call-start = ((), (), s32[]{:S(2)}) async-start(), calls=%async_computation.4 | async-start | bytes 2211840 | tf_op jit(solution)/shard_map/reduce_scatter | solution.py:114
  11.8 31.0 %copy-start.2 = (bf16[32,3072]{1,0:T(8,128)(2,1)S(1)}, bf16[32,3072]{1,0:T(8,128)(2,1)}, u32[]{:S(2)}) copy-start(bf16[32,3072]{1,0:T(8,128)(2,1)} %param.12) | copy-start | bytes 589828
  11.8 31.3 %copy-start = (bf16[256,3072]{1,0:T(8,128)(2,1)S(1)}, bf16[256,3072]{1,0:T(8,128)(2,1)}, u32[]{:S(2)}) copy-start(bf16[256,3072]{1,0:T(8,128)(2,1)} %param.11) | copy-start | bytes 4718596
  15.9 33.5 %copy-start.6 = (f32[2,2,4,128]{3,2,1,0:T(4,128)S(1)}, f32[2,2,4,128]{3,2,1,0:T(4,128)}, u32[]{:S(2)}) copy-start(f32[2,2,4,128]{3,2,1,0:T(4,128)} %param.19) | copy-start | bytes 24580
  353.2 1.2 copy-start.3
  355.7 30.4 %collective-permute-start = (bf16[288,1024]{1,0:T(8,128)(2,1)S(1)}, bf16[288,1024]{1,0:T(8,128)(2,1)S(1)}, u32[]{:S(2)}, u32[]{:S(2)}) collective-permute-start(bf16[288,1024]{1,0:T(8,128)(2,1)S(1)} %reshape.144), channel_id=1, source_target_pairs={{0,4},{4,8},{8,12},{12,0},{1,5},{5,9},{9,13},{13,1},{2,6},{6,10},{... | collective-permute-start | bytes 1769480 | tf_op jit(solution)/shard_map/ppermute | solution.py:75
  386.0 33.9 %collective-permute-start.1 = (bf16[288,1024]{1,0:T(8,128)(2,1)S(1)}, bf16[288,1024]{1,0:T(8,128)(2,1)S(1)}, u32[]{:S(2)}, u32[]{:S(2)}) collective-permute-start(bf16[288,1024]{1,0:T(8,128)(2,1)S(1)} %collective-permute-done), channel_id=1, source_target_pairs={{0,4},{4,8},{8,12},{12,0},{1,5},{5,9},{9,13},{13,1},{2,6},{6,10},{... | collective-permute-start | bytes 1769480 | tf_op jit(solution)/shard_map/ppermute | solution.py:75
  420.0 43.3 %collective-permute-start.2 = (bf16[288,1024]{1,0:T(8,128)(2,1)S(1)}, bf16[288,1024]{1,0:T(8,128)(2,1)S(1)}, u32[]{:S(2)}, u32[]{:S(2)}) collective-permute-start(bf16[288,1024]{1,0:T(8,128)(2,1)S(1)} %collective-permute-done.1), channel_id=1, source_target_pairs={{0,4},{4,8},{8,12},{12,0},{1,5},{5,9},{9,13},{13,1},{2,6},{6,10},{... | collective-permute-start | bytes 1769480 | tf_op jit(solution)/shard_map/ppermute | solution.py:75
  469.2 1.7 copy-start.1
Sparse Core Ops, SparseCore 0:
  9.6 170.1 all-gather.4
  181.3 165.1 all-gather.6
  348.0 151.1 all-gather.8
  506.1 27.4 reduce-scatter.1
